TPU v7x, 32 devices: a whole 2x2x4 slice. The times are simulated.
32 devices in a mesh: expert: 4 (over y, x), rep: 4 (over z), hid: 2 (over core).
Axes of the slice: x: 2, y: 2, z: 4, core: 2. Of those that a mesh axis runs over, the one named last changes fastest.
Arguments:
- calib_rows: bfloat16 [8192, 6144], P(('expert', 'rep'), 'hid'), may hold values from -6 to 6
- routes: int32 [8192, 2], P(('expert', 'rep')), may hold values from 0 to 7, all different within a row; in each aligned block of 512 rows (0 to 511, 512 to 1023, ...) at most 256 rows name the same one
- sketch_seed: int32 [6144, 512], P('hid'), may hold values from -1 to 1
- up_weight: bfloat16 [8, 6144, 16384], P('expert', 'hid', 'rep'), may hold values from -0.078125 to 0.078125
Outputs:
- projected: float32 [16384, 8, 512], P(('rep', 'hid'), 'expert')
Inputs may be any that keep to these rules, and one draw needn't show every extreme that they name: `routes`: each row names 2 different experts. In each aligned block of 512 rows no expert is named by more than 256 rows, and every expert is named somewhere.
All inputs are finite; a program needn't handle non-finite values.
Results may differ from a plain program's by a relative error of at most 0.0037.
Values may be sent and summed in bfloat16 or wider, within the bound.
No kernel may reach another device: no remote copies, remote signals or barrier semaphores. Data moves between devices by JAX's collectives and lax.ppermute only.
A program may use at most 192 MiB of HBM per device.

v0:
```python
import jax
import jax.numpy as jnp
from jax import lax
from jax.sharding import PartitionSpec as P

D = 6144
EXPERTS = 8
CAP = 256
damping = 0.25


def shards(calib_rows, routes, sketch_seed, up_weight):
    exp_local = up_weight.shape[0]
    signs_half = sketch_seed.astype(jnp.bfloat16)
    signs_full = sketch_seed.astype(jnp.float32)
    expert_ids = jnp.arange(EXPERTS, dtype=jnp.int32)
    member = jnp.sum((routes[:, :, None] == expert_ids[None, None, :]).astype(jnp.float32), axis=1)
    row_squares = jnp.sum(jnp.square(calib_rows.astype(jnp.float32)), axis=1)
    leader = (lax.axis_index("hid") == 0).astype(jnp.float32)
    counts, squares = lax.psum(
        (jnp.sum(member, axis=0) * leader, jnp.sum(member * row_squares[:, None], axis=0)),
        ("expert", "rep", "hid"),
    )
    flat_routes = routes.reshape(-1)
    one_hot = (flat_routes[:, None] == expert_ids[None, :]).astype(jnp.int32)
    before = jnp.cumsum(one_hot, axis=0) - one_hot
    slot_index = jnp.sum(before * one_hot, axis=1)
    repeated = jnp.repeat(calib_rows, routes.shape[1], axis=0)
    outgoing = jnp.zeros((EXPERTS, CAP, calib_rows.shape[1]), jnp.bfloat16)
    outgoing = outgoing.at[flat_routes, slot_index].set(repeated)
    outgoing = outgoing.reshape(lax.axis_size("expert"), exp_local, CAP, calib_rows.shape[1])
    rows_here = lax.all_to_all(outgoing, "expert", split_axis=0, concat_axis=2, tiled=True)[0]
    partial_value = jnp.einsum(
        "kmd,dr->kmr", rows_here, signs_half, preferred_element_type=jnp.float32
    )
    summed_rows = lax.psum(partial_value, "hid")
    masked = summed_rows.astype(jnp.bfloat16)
    partial_gram = jnp.einsum("kmd,kmr->kdr", rows_here, masked, preferred_element_type=jnp.float32)
    summed = lax.psum(partial_gram, "rep")
    first_expert = lax.axis_index("expert") * exp_local
    row_counts = lax.dynamic_slice_in_dim(counts, first_expert, exp_local)
    square_sums = lax.dynamic_slice_in_dim(squares, first_expert, exp_local)
    ridge = damping * square_sums / (row_counts * D)
    sketch = (
        summed / row_counts[:, None, None] + ridge[:, None, None] * signs_full[None, :, :]
    ).astype(jnp.bfloat16)
    return lax.psum_scatter(
        jnp.einsum("edf,edr->fer", up_weight, sketch, preferred_element_type=jnp.float32),
        "hid",
        scatter_dimension=0,
        tiled=True,
    )


def solution(mesh):
    in_specs = (
        P(("expert", "rep"), "hid"),
        P(("expert", "rep"), None),
        P("hid", None),
        P("expert", "hid", "rep"),
    )
    out_specs = P(("rep", "hid"), "expert", None)
    return jax.shard_map(shards, mesh=mesh, in_specs=in_specs, out_specs=out_specs, check_vma=False)
```

profile of v0, /device:TPU:0, one launch (start us, length us, event | category | flops | bytes accessed | tf_op | source)
XLA Modules:
  0.0 748.2 jit_solution(2252918654287226031)
XLA Ops:
  6.5 0.8 copy.22
  7.7 0.2 reshape.73
  7.9 2.3 reduce-window.6
  10.2 0.3 slice_reduce_fusion
  10.7 0.8 and_reduce_fusion
  11.5 0.7 multiply_reduce_fusion.2
  12.2 7.0 broadcast_in_dim.5
  19.3 13.6 %reshape.84 = bf16[1024,3072]{1,0:T(8,128)(2,1)} reshape(bf16[512,2,3072]{2,1,0:T(2,128)(2,1)} %broadcast_in_dim.5) | data formatting | bytes 12582912 | tf_op jit(solution)/shard_map/reshape | solution.py:28
  32.9 17.2 %scatter_custom_fusion = bf16[2048,3072]{1,0:T(8,128)(2,1)} fusion(s32[1024]{0:T(1024)S(1)} %broadcast_select_fusion, bf16[1024,3072]{1,0:T(8,128)(2,1)} %reshape.84, bf16[]{:T(256)} %constant.10.clone.1), kind=kCustom, calls=%fused_computation.3 | custom fusion | bytes 12583424
  50.0 144.0 %all_to_all.15 = bf16[4,2,256,3072]{3,2,1,0:T(8,128)(2,1)S(1)} all-to-all(bf16[4,2,256,3072]{3,2,1,0:T(8,128)(2,1)} %bitcast.35), channel_id=1, replica_groups=mesh['expert'=4,'rep'=4,'hid'=2] {'expert'}, dimensions={0} | all-to-all | bytes 25165824 | tf_op jit(solution)/shard_map/all_to_all | solution.py:32
  194.0 2.3 copy.25
  196.3 4.5 copy-done
  200.8 8.8 %fusion.5 = f32[2,1024,512]{2,1,0:T(8,128)} fusion(bf16[2,1024,3072]{2,1,0:T(8,128)(2,1)S(1)} %bitcast.37, s32[3072,512]{1,0:T(8,128)S(1)} %bitcast.40), kind=kOutput, calls=%fused_computation.9 | convolution fusion | flops 6444023808 | bytes 23068672 | tf_op jit(solution)/shard_map/kmd,dr->kmr/dot_general | solution.py:33
  209.6 14.9 %all-reduce.5 = bf16[2,1024,512]{2,1,0:T(8,128)(2,1)S(1)} all-reduce(f32[2,1024,512]{2,1,0:T(8,128)} %fusion.5), channel_id=1, replica_groups=mesh['expert'=4,'rep'=4,'hid'=2] {'hid'}, use_global_device_ids=true, to_apply=%region_4.0 | all-reduce | flops 1048576 | bytes 6291456 | tf_op jit(solution)/shard_map/psum | solution.py:36
  224.5 12.4 %fusion.14 = f32[2,3072,512]{2,1,0:T(8,128)} fusion(bf16[2,1024,3072]{2,1,0:T(8,128)(2,1)} %bitcast.38, bf16[2,1024,512]{2,1,0:T(8,128)(2,1)S(1)} %all-reduce.5), kind=kOutput, calls=%fused_computation.35 | convolution fusion | flops 6442450944 | bytes 27262976 | tf_op jit(solution)/shard_map/kmd,kmr->kdr/dot_general | solution.py:38
  237.0 0.6 copy-done.2
  237.7 1.1 copy-done.1
  238.8 0.7 multiply_reduce_fusion
  239.6 44.5 %all-reduce = (f32[8]{0:T(128)S(1)}, f32[8]{0:T(128)S(1)}) all-reduce(f32[8]{0:T(128)S(1)} %broadcast_multiply_fusion, f32[8]{0:T(128)S(1)} %multiply_reduce_fusion.1), channel_id=1, replica_groups=mesh['expert'=4,'rep'=4,'hid'=2] {'expert','rep','hid'}, use_global_device_ids=true, to_apply=%region_7.8 | all-reduce | flops 16 | bytes 128 | tf_op jit(solution)/shard_map/psum | solution.py:20
  284.1 6.3 convert_element_type.35
  290.4 373.7 %all-reduce.4.cloned.1.call-done = f32[2,3072,512]{2,1,0:T(8,128)} async-done(((f32[2,3072,512]{2,1,0:T(8,128)}), f32[2,3072,512]{2,1,0:T(8,128)}) %all-reduce.4.cloned.1.call-update) | async-done | bytes 12582928 | tf_op jit(solution)/shard_map/psum | solution.py:39
  664.2 40.0 %convolution_bitcast_fusion = f32[4096,2,512]{0,2,1:T(8,128)} fusion(bf16[2,3072,4096]{2,1,0:T(8,128)(2,1)} %param.7, f32[2,3072,512]{2,1,0:T(8,128)} %all-reduce.4.cloned.1.call-done, f32[3072,512]{1,0:T(8,128)} %convert_element_type.35, f32[2]{0:T(128)S(1)} %get-tuple-element.9, f32[2]{0:T(128)S(1)} %get-tuple-element.10), kind=kOutput, calls=%fused_computation.2 | convolution fusion | flops 25782386688 | bytes 85983248 | tf_op jit(solution)/shard_map/edf,edr->fer/dot_general | solution.py:48
  704.2 24.0 %reduce-scatter.2.cloned.1.call-done = f32[2048,2,512]{0,2,1:T(8,128)} async-done(((f32[4096,2,512]{0,2,1:T(8,128)}), f32[2048,2,512]{0,2,1:T(8,128)}) %reduce-scatter.2.cloned.1.call-update) | async-done | bytes 8388624 | tf_op jit(solution)/shard_map/reduce_scatter | solution.py:47
  728.2 13.1 %copy.28 = f32[2048,2,512]{2,1,0:T(2,128)} copy(f32[2048,2,512]{0,2,1:T(8,128)} %reduce-scatter.2.cloned.1.call-done) | data formatting | bytes 16777216 | tf_op jit(solution)/shard_map/reduce_scatter | solution.py:47
  (24 shorter events, 1.0 us)
Async XLA Ops:
  6.5 657.6 %all-reduce.4.cloned.1.call-start = ((), (), s32[]{:S(2)}) async-start(), calls=%async_computation.2 | async-start | bytes 25165824 | tf_op jit(solution)/shard_map/psum | solution.py:39
  50.0 150.7 %slice-start = ((s8[6291456]{0:T(1024)(128)(4,1)}), s8[4194304]{0:T(1024)(128)(4,1)S(1)}, s32[]{:S(2)}) async-start(s8[6291456]{0:T(1024)(128)(4,1)} %bitcast.39), calls=%async_computation.4 | async-start | bytes 8388608
  194.0 6.8 slice-start.1
  196.3 4.5 copy-start
  236.9 0.7 copy-start.2
  236.9 1.9 copy-start.1
  236.9 491.3 %reduce-scatter.2.cloned.1.call-start = ((), (), s32[]{:S(2)}) async-start(), calls=%async_computation.3 | async-start | bytes 25165824 | tf_op jit(solution)/shard_map/reduce_scatter | solution.py:47
Sparse Core Ops, SparseCore 0:
  237.0 427.0 all-reduce.3
  704.3 23.8 reduce-scatter.1
where the time goes:
time: 749 us; the launch traced here: 748 us
  waiting for transfers between devices  398 us (53%)
  blocking collectives  203 us (27%)
  matrix products  61.2 us (8%)
  local copies, waits for them, and re-layouts  61 us (8%)
  between operations  13.5 us (2%)
  other arithmetic  11.3 us (2%)
    psum x1, waiting for transfers between devices, shards(): summed = lax.psum(partial_gram, 'rep')  374 us
    all_to_all x1, blocking collectives, shards(): lax.all_to_all(outgoing, 'expert', split_axis=0, concat_axis=2, tiled=True)  144 us
    psum x1, blocking collectives, shards(): lax.psum((jnp.sum(member, axis=0) * leader, jnp.sum(member * row_squares[...  44.5 us
    dot_general x1, matrix products, shards(): jnp.einsum('edf,edr->fer', up_weight, sketch, preferred_element_type=jnp....  40 us
    unnamed x12, local copies, waits for them, and re-layouts  24.1 us
    reduce_scatter x1, waiting for transfers between devices, shards(): lax.psum_scatter(jnp.einsum('edf,edr->fer', up_weight, sketch, preferred_...  24 us
  transfers between devices with their start and end apart: 2, of which 2 were waited for; matrix products, arithmetic and copies ran while one was open for 1% of the time, Pallas kernels for 0%

commit v1 on v0

--- a/solution.py
+++ b/solution.py
@@ -36,7 +36,9 @@
     summed_rows = lax.psum(partial_value, "hid")
     masked = summed_rows.astype(jnp.bfloat16)
     partial_gram = jnp.einsum("kmd,kmr->kdr", rows_here, masked, preferred_element_type=jnp.float32)
-    summed = lax.psum(partial_gram, "rep")
+    summed = partial_gram
+    for hop in (1, 2):
+        summed = summed + lax.ppermute(summed, "rep", [(dev, dev ^ hop) for dev in range(4)])
     first_expert = lax.axis_index("expert") * exp_local
     row_counts = lax.dynamic_slice_in_dim(counts, first_expert, exp_local)
     square_sums = lax.dynamic_slice_in_dim(squares, first_expert, exp_local)

time: 749 us -> 1170 us (1.56)
  blocking collectives: 203 us -> 719 us
  waiting for transfers between devices: 398 us -> 295 us
    psum x1, blocking collectives: 44.5 us -> 560 us  [shards(): lax.psum((jnp.sum(member, axis=0) * leader, jnp.sum(member * row_squares[...]
    psum x1 -> x0, waiting for transfers between devices: 374 us -> none  [shards(): summed = lax.psum(partial_gram, 'rep')]
    ppermute x0 -> x2, waiting for transfers between devices: none -> 271 us  [shards(): lax.ppermute(summed, 'rep', [(dev, dev ^ hop) for dev in range(4)])]
  transfers between devices with their start and end apart: 2 -> 3, of which waited for: 2 -> 2; matrix products, arithmetic and copies ran while one was open for 1% -> 1% of each run, Pallas kernels for 0% -> 0%
where the time goes in v1:
time: 1170 us
  blocking collectives  719 us (61%)
  waiting for transfers between devices  295 us (25%)
  local copies, waits for them, and re-layouts  59.4 us (5%)
  matrix products  58.4 us (5%)
  other arithmetic  17.4 us (1%)
  between operations  13.5 us (1%)
    psum x1, blocking collectives, shards(): lax.psum((jnp.sum(member, axis=0) * leader, jnp.sum(member * row_squares[...  560 us
    ppermute x2, waiting for transfers between devices, shards(): lax.ppermute(summed, 'rep', [(dev, dev ^ hop) for dev in range(4)])  271 us
    all_to_all x1, blocking collectives, shards(): lax.all_to_all(outgoing, 'expert', split_axis=0, concat_axis=2, tiled=True)  144 us
    dot_general x1, matrix products, shards(): jnp.einsum('edf,edr->fer', up_weight, sketch, preferred_element_type=jnp....  40.2 us
    reduce_scatter x1, waiting for transfers between devices, shards(): lax.psum_scatter(jnp.einsum('edf,edr->fer', up_weight, sketch, preferred_...  24.5 us
  transfers between devices with their start and end apart: 3, of which 2 were waited for; matrix products, arithmetic and copies ran while one was open for 1% of the time, Pallas kernels for 0%

profile of v1, /device:TPU:0, one launch (start us, length us, event | category | flops | bytes accessed | tf_op | source)
XLA Modules:
  0.0 1167.8 jit_solution(6825678740568247530)
XLA Ops:
  6.5 0.8 copy.15
  7.9 2.3 reduce-window.6
  10.2 0.3 slice_reduce_fusion
  10.7 0.8 and_reduce_fusion
  11.5 0.7 multiply_reduce_fusion.2
  12.2 7.0 broadcast_in_dim.5
  19.3 13.6 %reshape.84 = bf16[1024,3072]{1,0:T(8,128)(2,1)} reshape(bf16[512,2,3072]{2,1,0:T(2,128)(2,1)} %broadcast_in_dim.5) | data formatting | bytes 12582912 | tf_op jit(solution)/shard_map/reshape | solution.py:28
  32.9 17.2 %scatter_custom_fusion = bf16[2048,3072]{1,0:T(8,128)(2,1)} fusion(s32[1024]{0:T(1024)S(1)} %broadcast_select_fusion, bf16[1024,3072]{1,0:T(8,128)(2,1)} %reshape.84, bf16[]{:T(256)} %constant.10.clone.1), kind=kCustom, calls=%fused_computation.3 | custom fusion | bytes 12583424
  50.0 144.0 %all_to_all.15 = bf16[4,2,256,3072]{3,2,1,0:T(8,128)(2,1)S(1)} all-to-all(bf16[4,2,256,3072]{3,2,1,0:T(8,128)(2,1)} %bitcast.35), channel_id=1, replica_groups=mesh['expert'=4,'rep'=4,'hid'=2] {'expert'}, dimensions={0} | all-to-all | bytes 25165824 | tf_op jit(solution)/shard_map/all_to_all | solution.py:32
  194.0 2.3 copy.18
  196.3 4.6 copy-done
  200.9 8.8 fusion.5
  209.7 14.9 %all-reduce.2 = bf16[2,1024,512]{2,1,0:T(8,128)(2,1)S(1)} all-reduce(f32[2,1024,512]{2,1,0:T(8,128)} %fusion.5), channel_id=1, replica_groups=mesh['expert'=4,'rep'=4,'hid'=2] {'hid'}, use_global_device_ids=true, to_apply=%region_4.0 | all-reduce | flops 1048576 | bytes 6291456 | tf_op jit(solution)/shard_map/psum | solution.py:36
  224.6 9.4 fusion.14
  234.0 1.8 collective-permute-start
  235.8 270.9 %collective-permute-done = f32[2,3072,512]{2,1,0:T(8,128)S(1)} collective-permute-done((f32[2,3072,512]{2,1,0:T(8,128)S(1)}, f32[2,3072,512]{2,1,0:T(8,128)S(1)}, u32[]{:S(2)}, u32[]{:S(2)}) %collective-permute-start) | collective-permute-done | bytes 12582944 | tf_op jit(solution)/shard_map/ppermute | solution.py:41
  506.7 6.1 add.51
  512.8 2.8 collective-permute-start.1
  515.6 0.7 multiply_reduce_fusion
  516.5 560.3 %all-reduce = (f32[8]{0:T(128)S(1)}, f32[8]{0:T(128)S(1)}) all-reduce(f32[8]{0:T(128)S(1)} %broadcast_multiply_fusion, f32[8]{0:T(128)S(1)} %multiply_reduce_fusion.1), channel_id=1, replica_groups=mesh['expert'=4,'rep'=4,'hid'=2] {'expert','rep','hid'}, use_global_device_ids=true, to_apply=%region_6.0 | all-reduce | flops 16 | bytes 128 | tf_op jit(solution)/shard_map/psum | solution.py:20
  1076.8 6.3 convert_element_type.35
  1083.1 40.2 %convolution_bitcast_fusion = f32[4096,2,512]{0,2,1:T(8,128)} fusion(bf16[2,3072,4096]{2,1,0:T(8,128)(2,1)} %param.7, f32[2,3072,512]{2,1,0:T(8,128)} %add.51, f32[2,3072,512]{2,1,0:T(8,128)} %collective-permute-done.1, f32[3072,512]{1,0:T(8,128)} %convert_element_type.35, f32[2]{0:T(128)S(1)} %get-tuple-element.9, f32[2]{0:T(128)S(1)} %get-tuple-element.10), kind=kOutput, calls=%fused_computation.2 | convolution fusion | flops 25785532416 | bytes 98566160 | tf_op jit(solution)/shard_map/edf,edr->fer/dot_general | solution.py:50
  1123.4 24.5 %reduce-scatter.2.cloned.1.call-done = f32[2048,2,512]{0,2,1:T(8,128)} async-done(((f32[4096,2,512]{0,2,1:T(8,128)}), f32[2048,2,512]{0,2,1:T(8,128)}) %reduce-scatter.2.cloned.1.call-update) | async-done | bytes 8388624 | tf_op jit(solution)/shard_map/reduce_scatter | solution.py:49
  1147.8 13.1 %copy.21 = f32[2048,2,512]{2,1,0:T(2,128)} copy(f32[2048,2,512]{0,2,1:T(8,128)} %reduce-scatter.2.cloned.1.call-done) | data formatting | bytes 16777216 | tf_op jit(solution)/shard_map/reduce_scatter | solution.py:49
  (26 shorter events, 1.2 us)
Async XLA Ops:
  6.5 1141.3 %reduce-scatter.2.cloned.1.call-start = ((), (), s32[]{:S(2)}) async-start(), calls=%async_computation.2 | async-start | bytes 25165824 | tf_op jit(solution)/shard_map/reduce_scatter | solution.py:49
  50.0 150.8 %slice-start = ((s8[6291456]{0:T(1024)(128)(4,1)}), s8[4194304]{0:T(1024)(128)(4,1)S(1)}, s32[]{:S(2)}) async-start(s8[6291456]{0:T(1024)(128)(4,1)} %bitcast.39), calls=%async_computation.3 | async-start | bytes 8388608
  194.0 6.9 slice-start.1
  196.3 4.6 copy-start
  234.0 281.5 %copy-start.2 = (s32[512,2]{0,1:T(2,128)S(1)}, s32[512,2]{0,1:T(2,128)}, u32[]{:S(2)}) copy-start(s32[512,2]{0,1:T(2,128)} %param.5) | copy-start | bytes 12292
  234.0 281.7 %copy-start.1 = (bf16[512,3072]{1,0:T(8,128)(2,1)S(1)}, bf16[512,3072]{1,0:T(8,128)(2,1)}, u32[]{:S(2)}) copy-start(bf16[512,3072]{1,0:T(8,128)(2,1)} %param.4) | copy-start | bytes 9437188
  234.0 272.7 %collective-permute-start = (f32[2,3072,512]{2,1,0:T(8,128)S(1)}, f32[2,3072,512]{2,1,0:T(8,128)S(1)}, u32[]{:S(2)}, u32[]{:S(2)}) collective-permute-start(f32[2,3072,512]{2,1,0:T(8,128)S(1)} %fusion.14), channel_id=1, source_target_pairs={{0,2},{2,0},{4,6},{6,4},{1,3},{3,1},{5,7},{7,5},{8,10},{10,8},{12,... | collective-permute-start | bytes 37748744 | tf_op jit(solution)/shard_map/ppermute | solution.py:41
  512.8 570.4 %collective-permute-start.1 = (f32[2,3072,512]{2,1,0:T(8,128)}, f32[2,3072,512]{2,1,0:T(8,128)}, u32[]{:S(2)}, u32[]{:S(2)}) collective-permute-start(f32[2,3072,512]{2,1,0:T(8,128)} %add.51), channel_id=1, source_target_pairs={{0,4},{2,6},{4,0},{6,2},{1,5},{3,7},{5,1},{7,3},{8,12},{10,14},{12... | collective-permute-start | bytes 37748744 | tf_op jit(solution)/shard_map/ppermute | solution.py:41
Sparse Core Ops, SparseCore 0:
  1123.5 24.2 reduce-scatter.1
